TPU v7x, 32 devices: a whole 2x2x4 slice. The times are simulated.
32 devices in a mesh: dp: 8 (over y, x, core), tensor: 4 (over z).
Axes of the slice: x: 2, y: 2, z: 4, core: 2. Of those that a mesh axis runs over, the one named last changes fastest.
Arguments:
- tokens: bfloat16 [256, 6144], P('dp', 'tensor'), may hold values from -6 to 6
- router_weight: bfloat16 [6144, 8], P('tensor'), may hold values from -0.078125 to 0.078125
- expert_ids: int32 [256, 2], P('dp'), may hold values from 0 to 7, all different within a row; in each aligned block of 32 rows (0 to 31, 32 to 63, ...) at most 12 rows name the same one
- w_gate: bfloat16 [8, 6144, 12288], P('dp', None, 'tensor'), may hold values from -0.078125 to 0.078125
- w_up: bfloat16 [8, 6144, 12288], P('dp', None, 'tensor'), may hold values from -0.078125 to 0.078125
- w_down: bfloat16 [8, 12288, 6144], P('dp', 'tensor'), may hold values from -0.0546875 to 0.0546875
Outputs:
- moe_out: bfloat16 [256, 6144], P('dp', 'tensor')
Inputs may be any that keep to these rules, and one draw needn't show every extreme that they name: `expert_ids`: the two experts of a token differ. In each aligned block of 32 rows (the rows of one index of dp) no expert is named by more than 12 rows, a bound that some blocks reach.
All inputs are finite; a program needn't handle non-finite values.
Results may differ from a plain program's by a relative error of at most 0.022.
Values may be sent and summed in bfloat16 or wider, within the bound.
A program may use at most 192 MiB of HBM per device.

v0:
```python
import jax
import jax.numpy as jnp
from jax import lax
from jax.sharding import PartitionSpec as P

EXPERTS = 8
CAP = 12


def per_device(tokens, router_weight, expert_ids, w_gate, w_up, w_down):
    tok_rows = tokens.shape[0]
    share = tokens.shape[1]
    dp_count = lax.axis_size("dp")
    groups = dp_count // EXPERTS
    slot_count = EXPERTS * CAP
    partial_value = jnp.dot(tokens, router_weight, preferred_element_type=jnp.float32)
    logits = lax.psum(partial_value, "tensor")
    choose = (expert_ids[:, :, None] == jnp.arange(EXPERTS, dtype=jnp.int32)[None, None, :]).astype(
        jnp.float32
    )
    chosen = jnp.sum(choose * logits[:, None, :], axis=2)
    first = jax.nn.sigmoid(chosen[:, 0] - chosen[:, 1])
    gates = jnp.stack([first, 1.0 - first], axis=1)
    flat = expert_ids.reshape(-1)
    onehot = (flat[:, None] == jnp.arange(EXPERTS, dtype=jnp.int32)[None, :]).astype(jnp.int32)
    ranks = jnp.sum((jnp.cumsum(onehot, axis=0) - onehot) * onehot, axis=1)
    position = flat * CAP + ranks
    slot_table = (position[:, None] == jnp.arange(slot_count, dtype=jnp.int32)[None, :]).astype(
        jnp.float32
    )
    slot_table = slot_table.reshape(tok_rows, 2, slot_count)
    placing = jnp.sum(slot_table, axis=1).astype(jnp.bfloat16)
    weights = jnp.sum(slot_table * gates[:, :, None], axis=1)
    packed = lax.dot_general(
        placing, tokens, (((0,), (0,)), ((), ())), preferred_element_type=jnp.float32
    ).astype(jnp.bfloat16)
    outgoing = jnp.broadcast_to(
        packed.reshape(EXPERTS, 1, CAP, share), (EXPERTS, groups, CAP, share)
    ).reshape(dp_count, CAP, share)
    incoming = lax.all_to_all(outgoing, "dp", split_axis=0, concat_axis=0, tiled=True)
    rows = incoming.reshape(dp_count * CAP, share)
    gate_w = w_gate[0]
    up_w = w_up[0]
    down_w = w_down[0]
    whole = lax.all_gather(rows, "tensor", axis=1, tiled=True)
    gate = jnp.dot(whole, gate_w, preferred_element_type=jnp.float32)
    up = jnp.dot(whole, up_w, preferred_element_type=jnp.float32)
    hidden = (jax.nn.silu(gate) * up).astype(jnp.bfloat16)
    terms = jnp.dot(hidden, down_w, preferred_element_type=jnp.float32)
    summed = lax.psum_scatter(terms.astype(jnp.bfloat16), "tensor", scatter_dimension=1, tiled=True)
    leaving = summed.reshape(dp_count, CAP, share)
    back = lax.all_to_all(leaving, "dp", split_axis=0, concat_axis=0, tiled=True)
    merged = jnp.sum(back.astype(jnp.float32).reshape(EXPERTS, groups, CAP, share), axis=1).reshape(
        slot_count, share
    )
    result = jnp.dot(
        weights, merged, precision=lax.Precision.HIGHEST, preferred_element_type=jnp.float32
    )
    return result.astype(jnp.bfloat16)


def solution(mesh):
    return jax.shard_map(
        per_device,
        mesh=mesh,
        in_specs=(
            P("dp", "tensor"),
            P("tensor", None),
            P("dp", None),
            P("dp", None, "tensor"),
            P("dp", None, "tensor"),
            P("dp", "tensor", None),
        ),
        out_specs=P("dp", "tensor"),
        check_vma=False,
    )
```

profile of v0, /device:TPU:0, one launch (start us, length us, event | category | flops | bytes accessed | tf_op | source)
XLA Modules:
  0.0 160.2 jit_solution(1804313521024078486)
XLA Ops:
  6.5 0.9 copy-done
  7.4 0.9 fusion.21
  8.3 13.5 %psum.7 = f32[32,8]{0,1:T(8,128)S(1)} all-reduce(f32[32,8]{0,1:T(8,128)S(1)} %fusion.21), channel_id=1, replica_groups=mesh['dp'=8,'tensor'=4] {'tensor'}, use_global_device_ids=true, to_apply=%region_2.0 | all-reduce | flops 256 | bytes 2048 | tf_op jit(solution)/shard_map/psum | solution.py:17
  21.8 0.8 copy.27
  22.5 0.7 select_reduce_fusion.2
  23.2 0.1 eq.42
  23.3 0.1 fusion.18
  23.4 0.1 reduce_window_sum.11
  23.5 0.2 select_reduce_fusion.1
  23.7 0.1 reduce_sum.43
  23.8 0.1 copy.28
  23.9 0.7 multiply_add_fusion
  24.6 0.1 convert_reduce_fusion
  24.7 0.3 convolution_convert_fusion
  25.0 0.1 reshape_reshape.3
  25.0 11.8 %all_to_all.10 = bf16[8,12,1536]{2,1,0:T(8,128)(2,1)S(1)} all-to-all(bf16[8,12,1536]{2,1,0:T(8,128)(2,1)S(1)} %reshape_reshape.3), channel_id=1, replica_groups=mesh['dp'=8,'tensor'=4] {'dp'}, dimensions={0} | all-to-all | bytes 589824 | tf_op jit(solution)/shard_map/all_to_all | solution.py:40
  36.8 0.8 reshape.35
  37.7 26.7 %all-gather.2.cloned.1.call-done = bf16[96,6144]{1,0:T(8,128)(2,1)} async-done(((bf16[96,1536]{1,0:T(8,128)(2,1)}), bf16[96,6144]{1,0:T(8,128)(2,1)}) %all-gather.2.cloned.1.call-update) | async-done | bytes 1179664 | tf_op jit(solution)/shard_map/all_gather | solution.py:45
  64.4 18.4 %fusion.4 = f32[96,3072]{1,0:T(8,128)S(1)} fusion(bf16[96,6144]{1,0:T(8,128)(2,1)} %all-gather.2.cloned.1.call-done, bf16[1,6144,3072]{2,1,0:T(8,128)(2,1)} %param.9), kind=kOutput, calls=%fused_computation.4 | convolution fusion | flops 3623878656 | bytes 40108032 | tf_op jit(solution)/shard_map/dot_general | solution.py:46
  82.8 28.1 %fusion.6 = bf16[96,6144]{1,0:T(8,128)(2,1)} fusion(bf16[1,3072,6144]{2,1,0:T(8,128)(2,1)} %param.11, bf16[96,6144]{1,0:T(8,128)(2,1)S(1)} %copy-done.2, bf16[1,6144,3072]{2,1,0:T(8,128)(2,1)} %param.10, f32[96,3072]{1,0:T(8,128)S(1)} %fusion.4), kind=kOutput, calls=%fused_computation.6 | convolution fusion | flops 7250116608 | bytes 79036416 | tf_op jit(solution)/shard_map/dot_general | solution.py:49
  110.9 28.7 %reduce-scatter.2.cloned.1.call-done = bf16[96,1536]{1,0:T(8,128)(2,1)} async-done(((bf16[96,6144]{1,0:T(8,128)(2,1)}), bf16[96,1536]{1,0:T(8,128)(2,1)}) %reduce-scatter.2.cloned.1.call-update) | async-done | bytes 294928 | tf_op jit(solution)/shard_map/reduce_scatter | solution.py:50
  139.6 1.0 reshape.36
  140.7 11.8 %all_to_all.11 = bf16[8,12,1536]{2,1,0:T(8,128)(2,1)S(1)} all-to-all(bf16[8,12,1536]{2,1,0:T(8,128)(2,1)S(1)} %reshape.36), channel_id=1, replica_groups=mesh['dp'=8,'tensor'=4] {'dp'}, dimensions={0} | all-to-all | bytes 589824 | tf_op jit(solution)/shard_map/all_to_all | solution.py:52
  152.5 0.9 convolution_convert_fusion.1
  (12 shorter events, 0.2 us)
Async XLA Ops:
  6.5 0.9 copy-start
  6.5 57.9 %all-gather.2.cloned.1.call-start = ((), (), s32[]{:S(2)}) async-start(), calls=%async_computation.3 | async-start | bytes 1474560 | tf_op jit(solution)/shard_map/all_gather | solution.py:45
  37.7 102.0 %reduce-scatter.2.cloned.1.call-start = ((), (), s32[]{:S(2)}) async-start(), calls=%async_computation.4 | async-start | bytes 1474560 | tf_op jit(solution)/shard_map/reduce_scatter | solution.py:50
  64.4 18.4 %copy-start.2 = (bf16[96,6144]{1,0:T(8,128)(2,1)S(1)}, bf16[96,6144]{1,0:T(8,128)(2,1)}, u32[]{:S(2)}) copy-start(bf16[96,6144]{1,0:T(8,128)(2,1)} %all-gather.2.cloned.1.call-done) | copy-start | bytes 3538948
  110.9 42.5 %copy-start.1 = (bf16[32,1536]{1,0:T(8,128)(2,1)S(1)}, bf16[32,1536]{1,0:T(8,128)(2,1)}, u32[]{:S(2)}) copy-start(bf16[32,1536]{1,0:T(8,128)(2,1)} %param.6) | copy-start | bytes 294916
Sparse Core Ops, SparseCore 0:
  37.8 26.5 all-gather.1
  111.0 28.5 reduce-scatter.1
where the time goes:
time: 161 us; the launch traced here: 160 us
  waiting for transfers between devices  55.4 us (34%)
  matrix products  48.5 us (30%)
  blocking collectives  37 us (23%)
  between operations  13.5 us (8%)
  local copies, waits for them, and re-layouts  3.9 us (2%)
  other arithmetic  1.85 us (1%)
    reduce_scatter x1, waiting for transfers between devices, per_device(): lax.psum_scatter(terms.astype(jnp.bfloat16), 'tensor', scatter_dimension=...  28.7 us
    dot_general x1, matrix products, per_device(): terms = jnp.dot(hidden, down_w, preferred_element_type=jnp.float32)  28.1 us
    all_gather x1, waiting for transfers between devices, per_device(): whole = lax.all_gather(rows, 'tensor', axis=1, tiled=True)  26.7 us
    dot_general x1, matrix products, per_device(): gate = jnp.dot(whole, gate_w, preferred_element_type=jnp.float32)  18.4 us
    psum x1, blocking collectives, per_device(): logits = lax.psum(partial_value, 'tensor')  13.5 us
    all_to_all x1, blocking collectives, per_device(): lax.all_to_all(outgoing, 'dp', split_axis=0, concat_axis=0, tiled=True)  11.8 us
    all_to_all x1, blocking collectives, per_device(): lax.all_to_all(leaving, 'dp', split_axis=0, concat_axis=0, tiled=True)  11.8 us
  transfers between devices with their start and end apart: 2, of which 2 were waited for; matrix products, arithmetic and copies ran while one was open for 0% of the time, Pallas kernels for 0%

commit v1 on v0

--- a/solution.py
+++ b/solution.py
@@ -37,7 +37,18 @@
     outgoing = jnp.broadcast_to(
         packed.reshape(EXPERTS, 1, CAP, share), (EXPERTS, groups, CAP, share)
     ).reshape(dp_count, CAP, share)
-    incoming = lax.all_to_all(outgoing, "dp", split_axis=0, concat_axis=0, tiled=True)
+    ways, here = (lax.axis_size("dp"), lax.axis_index("dp"))
+    width = outgoing.shape[0] // ways
+    shape = list(outgoing.shape)
+    shape[0] = width
+    height = shape[0]
+    shape[0] = height * ways
+    incoming = jnp.zeros(shape, outgoing.dtype)
+    for mask in range(ways):
+        part = lax.dynamic_slice_in_dim(outgoing, (here ^ mask) * width, width, axis=0)
+        if mask:
+            part = lax.ppermute(part, "dp", [(d, d ^ mask) for d in range(ways)])
+        incoming = lax.dynamic_update_slice_in_dim(incoming, part, (here ^ mask) * height, axis=0)
     rows = incoming.reshape(dp_count * CAP, share)
     gate_w = w_gate[0]
     up_w = w_up[0]

time: 161 us -> 163 us (1.012)
  blocking collectives: 37 us -> 25.2 us
  waiting for transfers between devices: 55.4 us -> 63 us
  starting transfers between devices: 0.04 us -> 6.72 us
    all_to_all x1 -> x0, blocking collectives: 11.8 us -> none  [per_device(): lax.all_to_all(outgoing, 'dp', split_axis=0, concat_axis=0, tiled=True)]
    ppermute x0 -> x7, starting transfers between devices: none -> 6.67 us  [per_device(): part = lax.ppermute(part, 'dp', [(d, d ^ mask) for d in range(ways)])]
    ppermute x0 -> x7, waiting for transfers between devices: none -> 6.04 us  [per_device(): part = lax.ppermute(part, 'dp', [(d, d ^ mask) for d in range(ways)])]
  transfers between devices with their start and end apart: 2 -> 9, of which waited for: 2 -> 4; matrix products, arithmetic and copies ran while one was open for 0% -> 0% of each run, Pallas kernels for 0% -> 0%
where the time goes in v1:
time: 163 us
  waiting for transfers between devices  63 us (39%)
  matrix products  48.3 us (30%)
  blocking collectives  25.2 us (15%)
  between operations  13.6 us (8%)
  starting transfers between devices  6.72 us (4%)
  local copies, waits for them, and re-layouts  4.04 us (2%)
  other arithmetic  1.85 us (1%)
    reduce_scatter x1, waiting for transfers between devices, per_device(): lax.psum_scatter(terms.astype(jnp.bfloat16), 'tensor', scatter_dimension=...  28.7 us
    all_gather x1, waiting for transfers between devices, per_device(): whole = lax.all_gather(rows, 'tensor', axis=1, tiled=True)  28.3 us
    dot_general x1, matrix products, per_device(): terms = jnp.dot(hidden, down_w, preferred_element_type=jnp.float32)  28.1 us
    dot_general x1, matrix products, per_device(): up = jnp.dot(whole, up_w, preferred_element_type=jnp.float32)  18.2 us
    psum x1, blocking collectives, per_device(): logits = lax.psum(partial_value, 'tensor')  13.5 us
    all_to_all x1, blocking collectives, per_device(): lax.all_to_all(leaving, 'dp', split_axis=0, concat_axis=0, tiled=True)  11.8 us
    ppermute x7, starting transfers between devices, per_device(): part = lax.ppermute(part, 'dp', [(d, d ^ mask) for d in range(ways)])  6.67 us
    ppermute x7, waiting for transfers between devices, per_device(): part = lax.ppermute(part, 'dp', [(d, d ^ mask) for d in range(ways)])  6.04 us
  transfers between devices with their start and end apart: 9, of which 4 were waited for; matrix products, arithmetic and copies ran while one was open for 0% of the time, Pallas kernels for 0%

profile of v1, /device:TPU:0, one launch (start us, length us, event | category | flops | bytes accessed | tf_op | source)
XLA Modules:
  0.0 162.8 jit_solution(7742500097044477660)
XLA Ops:
  6.5 0.9 copy-done
  7.4 0.9 fusion.17
  8.3 13.5 %psum.7 = f32[32,8]{0,1:T(8,128)S(1)} all-reduce(f32[32,8]{0,1:T(8,128)S(1)} %fusion.17), channel_id=1, replica_groups=mesh['dp'=8,'tensor'=4] {'tensor'}, use_global_device_ids=true, to_apply=%region_2.0 | all-reduce | flops 256 | bytes 2048 | tf_op jit(solution)/shard_map/psum | solution.py:17
  21.8 0.8 copy.27
  22.5 0.7 select_reduce_fusion.2
  23.5 0.2 select_reduce_fusion.1
  23.9 0.7 multiply_add_fusion
  24.7 0.3 convolution_convert_fusion
  25.2 2.5 %collective-permute-start.6 = (bf16[1,12,1536]{2,1,0:T(8,128)(2,1)S(1)}, bf16[1,12,1536]{2,1,0:T(8,128)(2,1)S(1)}, u32[]{:S(2)}, u32[]{:S(2)}) collective-permute-start(bf16[1,12,1536]{2,1,0:T(8,128)(2,1)S(1)} %get-tuple-element.9), channel_id=1, source_target_pairs={{0,28},{4,24},{8,20},{12,16},{16,12},{20,8},{24,4},{28,0},{1,29},{... | collective-permute-start | bytes 110600 | tf_op jit(solution)/shard_map/ppermute | solution.py:50
  27.8 0.5 collective-permute-start.5
  28.3 0.9 collective-permute-start.4
  29.2 0.6 collective-permute-start.3
  29.8 1.5 collective-permute-start.1
  31.3 2.6 %collective-permute-done.1 = bf16[1,12,1536]{2,1,0:T(8,128)(2,1)S(1)} collective-permute-done((bf16[1,12,1536]{2,1,0:T(8,128)(2,1)S(1)}, bf16[1,12,1536]{2,1,0:T(8,128)(2,1)S(1)}, u32[]{:S(2)}, u32[]{:S(2)}) %collective-permute-start.1) | collective-permute-done | bytes 36896 | tf_op jit(solution)/shard_map/ppermute | solution.py:50
  33.9 0.6 collective-permute-start.2
  34.5 3.4 %collective-permute-done.2 = bf16[1,12,1536]{2,1,0:T(8,128)(2,1)S(1)} collective-permute-done((bf16[1,12,1536]{2,1,0:T(8,128)(2,1)S(1)}, bf16[1,12,1536]{2,1,0:T(8,128)(2,1)S(1)}, u32[]{:S(2)}, u32[]{:S(2)}) %collective-permute-start.2) | collective-permute-done | bytes 36896 | tf_op jit(solution)/shard_map/ppermute | solution.py:50
  38.0 0.8 reshape.35
  38.9 28.3 %all-gather.2.cloned.1.call-done = bf16[96,6144]{1,0:T(8,128)(2,1)} async-done(((bf16[96,1536]{1,0:T(8,128)(2,1)}), bf16[96,6144]{1,0:T(8,128)(2,1)}) %all-gather.2.cloned.1.call-update) | async-done | bytes 1179664 | tf_op jit(solution)/shard_map/all_gather | solution.py:56
  67.1 18.2 %fusion.2 = f32[96,3072]{1,0:T(8,128)S(1)} fusion(bf16[96,6144]{1,0:T(8,128)(2,1)} %all-gather.2.cloned.1.call-done, bf16[1,6144,3072]{2,1,0:T(8,128)(2,1)} %param.10), kind=kOutput, calls=%fused_computation.2 | convolution fusion | flops 3623878656 | bytes 40108032 | tf_op jit(solution)/shard_map/dot_general | solution.py:58
  85.4 28.1 %fusion.6 = bf16[96,6144]{1,0:T(8,128)(2,1)} fusion(bf16[1,3072,6144]{2,1,0:T(8,128)(2,1)} %param.11, f32[96,3072]{1,0:T(8,128)S(1)} %fusion.2, bf16[96,6144]{1,0:T(8,128)(2,1)S(1)} %copy-done.2, bf16[1,6144,3072]{2,1,0:T(8,128)(2,1)} %param.9), kind=kOutput, calls=%fused_computation.6 | convolution fusion | flops 7250116608 | bytes 79036416 | tf_op jit(solution)/shard_map/dot_general | solution.py:60
  113.5 28.7 %reduce-scatter.2.cloned.1.call-done = bf16[96,1536]{1,0:T(8,128)(2,1)} async-done(((bf16[96,6144]{1,0:T(8,128)(2,1)}), bf16[96,1536]{1,0:T(8,128)(2,1)}) %reduce-scatter.2.cloned.1.call-update) | async-done | bytes 294928 | tf_op jit(solution)/shard_map/reduce_scatter | solution.py:61
  142.2 1.0 reshape.36
  143.2 11.8 %all_to_all.5 = bf16[8,12,1536]{2,1,0:T(8,128)(2,1)S(1)} all-to-all(bf16[8,12,1536]{2,1,0:T(8,128)(2,1)S(1)} %reshape.36), channel_id=1, replica_groups=mesh['dp'=8,'tensor'=4] {'dp'}, dimensions={0} | all-to-all | bytes 589824 | tf_op jit(solution)/shard_map/all_to_all | solution.py:63
  155.0 0.9 convolution_convert_fusion.1
  (34 shorter events, 1.0 us)
Async XLA Ops:
  6.5 0.9 copy-start
  6.5 60.6 %all-gather.2.cloned.1.call-start = ((), (), s32[]{:S(2)}) async-start(), calls=%async_computation.2 | async-start | bytes 1474560 | tf_op jit(solution)/shard_map/all_gather | solution.py:56
  25.2 4.6 %collective-permute-start = (bf16[1,12,1536]{2,1,0:T(8,128)(2,1)S(1)}, bf16[1,12,1536]{2,1,0:T(8,128)(2,1)S(1)}, u32[]{:S(2)}, u32[]{:S(2)}) collective-permute-start(bf16[1,12,1536]{2,1,0:T(8,128)(2,1)S(1)} %get-tuple-element.15), channel_id=1, source_target_pairs={{0,4},{4,0},{8,12},{12,8},{16,20},{20,16},{24,28},{28,24},{1,5},{5... | collective-permute-start | bytes 110600 | tf_op jit(solution)/shard_map/ppermute | solution.py:50
  25.2 12.7 %collective-permute-start.6 = (bf16[1,12,1536]{2,1,0:T(8,128)(2,1)S(1)}, bf16[1,12,1536]{2,1,0:T(8,128)(2,1)S(1)}, u32[]{:S(2)}, u32[]{:S(2)}) collective-permute-start(bf16[1,12,1536]{2,1,0:T(8,128)(2,1)S(1)} %get-tuple-element.9), channel_id=1, source_target_pairs={{0,28},{4,24},{8,20},{12,16},{16,12},{20,8},{24,4},{28,0},{1,29},{... | collective-permute-start | bytes 110600 | tf_op jit(solution)/shard_map/ppermute | solution.py:50
  27.8 10.2 %collective-permute-start.5 = (bf16[1,12,1536]{2,1,0:T(8,128)(2,1)S(1)}, bf16[1,12,1536]{2,1,0:T(8,128)(2,1)S(1)}, u32[]{:S(2)}, u32[]{:S(2)}) collective-permute-start(bf16[1,12,1536]{2,1,0:T(8,128)(2,1)S(1)} %get-tuple-element.10), channel_id=1, source_target_pairs={{0,24},{4,28},{8,16},{12,20},{16,8},{20,12},{24,0},{28,4},{1,25},{... | collective-permute-start | bytes 110600 | tf_op jit(solution)/shard_map/ppermute | solution.py:50
  28.3 9.7 %collective-permute-start.4 = (bf16[1,12,1536]{2,1,0:T(8,128)(2,1)S(1)}, bf16[1,12,1536]{2,1,0:T(8,128)(2,1)S(1)}, u32[]{:S(2)}, u32[]{:S(2)}) collective-permute-start(bf16[1,12,1536]{2,1,0:T(8,128)(2,1)S(1)} %get-tuple-element.11), channel_id=1, source_target_pairs={{0,20},{4,16},{8,28},{12,24},{16,4},{20,0},{24,12},{28,8},{1,21},{... | collective-permute-start | bytes 110600 | tf_op jit(solution)/shard_map/ppermute | solution.py:50
  29.2 8.7 %collective-permute-start.3 = (bf16[1,12,1536]{2,1,0:T(8,128)(2,1)S(1)}, bf16[1,12,1536]{2,1,0:T(8,128)(2,1)S(1)}, u32[]{:S(2)}, u32[]{:S(2)}) collective-permute-start(bf16[1,12,1536]{2,1,0:T(8,128)(2,1)S(1)} %get-tuple-element.12), channel_id=1, source_target_pairs={{0,16},{4,20},{8,24},{12,28},{16,0},{20,4},{24,8},{28,12},{1,17},{... | collective-permute-start | bytes 110600 | tf_op jit(solution)/shard_map/ppermute | solution.py:50
  29.8 4.1 %collective-permute-start.1 = (bf16[1,12,1536]{2,1,0:T(8,128)(2,1)S(1)}, bf16[1,12,1536]{2,1,0:T(8,128)(2,1)S(1)}, u32[]{:S(2)}, u32[]{:S(2)}) collective-permute-start(bf16[1,12,1536]{2,1,0:T(8,128)(2,1)S(1)} %get-tuple-element.14), channel_id=1, source_target_pairs={{0,8},{4,12},{8,0},{12,4},{16,24},{20,28},{24,16},{28,20},{1,9},{5... | collective-permute-start | bytes 110600 | tf_op jit(solution)/shard_map/ppermute | solution.py:50
  33.9 4.0 %collective-permute-start.2 = (bf16[1,12,1536]{2,1,0:T(8,128)(2,1)S(1)}, bf16[1,12,1536]{2,1,0:T(8,128)(2,1)S(1)}, u32[]{:S(2)}, u32[]{:S(2)}) collective-permute-start(bf16[1,12,1536]{2,1,0:T(8,128)(2,1)S(1)} %get-tuple-element.13), channel_id=1, source_target_pairs={{0,12},{4,8},{8,4},{12,0},{16,28},{20,24},{24,20},{28,16},{1,13},{... | collective-permute-start | bytes 110600 | tf_op jit(solution)/shard_map/ppermute | solution.py:50
  38.8 103.4 %reduce-scatter.2.cloned.1.call-start = ((), (), s32[]{:S(2)}) async-start(), calls=%async_computation.3 | async-start | bytes 1474560 | tf_op jit(solution)/shard_map/reduce_scatter | solution.py:61
  67.1 18.2 %copy-start.2 = (bf16[96,6144]{1,0:T(8,128)(2,1)S(1)}, bf16[96,6144]{1,0:T(8,128)(2,1)}, u32[]{:S(2)}) copy-start(bf16[96,6144]{1,0:T(8,128)(2,1)} %all-gather.2.cloned.1.call-done) | copy-start | bytes 3538948
  113.5 42.5 %copy-start.1 = (bf16[32,1536]{1,0:T(8,128)(2,1)S(1)}, bf16[32,1536]{1,0:T(8,128)(2,1)}, u32[]{:S(2)}) copy-start(bf16[32,1536]{1,0:T(8,128)(2,1)} %param.6) | copy-start | bytes 294916
Sparse Core Ops, SparseCore 0:
  38.9 28.1 all-gather.1
  113.6 28.5 reduce-scatter.1
